TPU v7x, 32 devices: a whole 2x2x4 slice. The times are simulated.
32 devices in a mesh: dp: 4 (over z), rows: 8 (over y, x, core).
Axes of the slice: x: 2, y: 2, z: 4, core: 2. Of those that a mesh axis runs over, the one named last changes fastest.
Arguments:
- latent: bfloat16 [8, 8, 64, 640], P('dp', 'rows'), may hold values from -16.25 to 16.25
- hidden: bfloat16 [8, 8, 64, 640], P('dp', 'rows'), may hold values from -16.25 to 16.25
- cotangent: bfloat16 [8, 8, 64, 640], P('dp', 'rows'), may hold values from -6 to 6
- filter_one: bfloat16 [9, 640, 640], P(None, 'dp', 'rows'), may hold values from -0.078125 to 0.078125
- filter_two: bfloat16 [9, 640, 640], P(None, 'dp', 'rows'), may hold values from -0.078125 to 0.078125
- gain_one: float32 [640], replicated, may hold values from 0.1 to 1.9
- shift_one: float32 [640], replicated, may hold values from -2.5 to 2.5
- gain_two: float32 [640], replicated, may hold values from 0.1 to 1.9
- shift_two: float32 [640], replicated, may hold values from -2.5 to 2.5
Outputs:
- latent_grad: bfloat16 [8, 8, 64, 640], P('dp', 'rows')
All inputs are finite; a program needn't handle non-finite values.
Results may differ from a plain program's by a relative error of at most 0.0027.
Values may be sent and summed in bfloat16 or wider, within the bound.
A program may use at most 128 MiB of HBM per device.

v0:
```python
import jax
import jax.numpy as jnp
from jax import lax
from jax.sharding import PartitionSpec as P

GROUPS = 16
GSIZE = 40


def extended(block, sides, width):
    for axis, dim in sides:
        count = lax.axis_size(axis)
        forward = [(i, i + 1) for i in range(count - 1)]
        backward = [(target, source) for source, target in forward]
        low = lax.ppermute(
            lax.slice_in_dim(block, block.shape[dim] - width, None, axis=dim), axis, forward
        )
        high = lax.ppermute(lax.slice_in_dim(block, 0, width, axis=dim), axis, backward)
        block = jnp.concatenate([low, block, high], axis=dim)
    return block


def group_sums(values):
    per_channel = jnp.sum(values, axis=(1, 2))
    return jnp.sum(per_channel.reshape(per_channel.shape[0], GROUPS, -1), axis=2)


def expand_groups(moment):
    return jnp.repeat(moment, GSIZE, axis=1)[:, None, None, :]


def finish_stats(sum_plain, sum_square, number):
    average = sum_plain / number
    variance = sum_square / number - average * average
    return (average, lax.rsqrt(variance + 1e-05))


def reduced_stats(field, number):
    values = field.astype(jnp.float32)
    sum_plain, sum_square = lax.psum((group_sums(values), group_sums(values * values)), "rows")
    return finish_stats(sum_plain, sum_square, number)


def norm_backward(field, stats, gain, shift, incoming, number):
    average, inverse = stats
    values = field.astype(jnp.float32)
    normed = (values - expand_groups(average)) * expand_groups(inverse)
    linear = normed * gain + shift
    logistic = jax.nn.sigmoid(linear)
    scaled = incoming * logistic * (1.0 + linear * (1.0 - logistic)) * gain
    sum_first, sum_second = lax.psum((group_sums(scaled), group_sums(scaled * normed)), "rows")
    first = sum_first / number
    second = sum_second / number
    return expand_groups(inverse) * (scaled - expand_groups(first) - normed * expand_groups(second))


def conv_backward(gradient, weights):
    images, rows_here, breadth, channels = gradient.shape
    padded = extended(gradient, (("rows", 1),), 1)
    padded = jnp.pad(padded, ((0, 0), (0, 0), (1, 1), (0, 0)))
    pixels = images * rows_here * breadth
    shifted = []
    for tap_index in range(9):
        down_step = tap_index // 3 - 1
        side_step = tap_index % 3 - 1
        window = padded[
            :, 1 - down_step : 1 - down_step + rows_here, 1 - side_step : 1 - side_step + breadth, :
        ]
        shifted.append(window.reshape(pixels, channels))
    stacked = jnp.stack(shifted, axis=1)
    gathered = lax.all_gather(weights, "dp", axis=1, tiled=True)
    section = lax.all_gather(gathered, "rows", axis=2, tiled=True)
    columns = section.shape[2]
    window = stacked.reshape(pixels, 9 * columns)
    flat = jnp.transpose(section, (0, 2, 1)).reshape(9 * columns, section.shape[1])
    result = jnp.dot(window, flat, preferred_element_type=jnp.float32)
    return result.reshape(images, rows_here, breadth, channels)


def body(
    latent, hidden, cotangent, filter_one, filter_two, gain_one, shift_one, gain_two, shift_two
):
    number = latent.shape[1] * lax.axis_size("rows") * latent.shape[2] * GSIZE
    stats_two = reduced_stats(hidden, number)
    back_two = conv_backward(cotangent, filter_two)
    hidden_grad = norm_backward(hidden, stats_two, gain_two, shift_two, back_two, number).astype(
        jnp.bfloat16
    )
    stats_one = reduced_stats(latent, number)
    back_one = conv_backward(hidden_grad, filter_one)
    latent_part = norm_backward(latent, stats_one, gain_one, shift_one, back_one, number)
    return (cotangent.astype(jnp.float32) + latent_part).astype(jnp.bfloat16)


def solution(mesh):
    in_specs = (
        P("dp", "rows", None, None),
        P("dp", "rows", None, None),
        P("dp", "rows", None, None),
        P(None, "dp", "rows"),
        P(None, "dp", "rows"),
        P(),
        P(),
        P(),
        P(),
    )
    out_specs = P("dp", "rows", None, None)
    return jax.shard_map(body, mesh=mesh, in_specs=in_specs, out_specs=out_specs, check_vma=False)
```

profile of v0, /device:TPU:28, one launch (start us, length us, event | category | flops | bytes accessed | tf_op | source)
XLA Modules:
  0.0 223.1 jit_solution(1200964164859489196)
XLA Ops:
  6.5 1.2 copy.112
  7.7 47.0 %all_gather.12 = bf16[9,640,80]{2,0,1:T(8,128)(2,1)S(1)} all-gather(bf16[9,160,80]{2,0,1:T(8,128)(2,1)S(1)} %copy.112), channel_id=1, replica_groups=mesh['dp'=4,'rows'=8] {'dp'}, dimensions={1}, use_global_device_ids=true | all-gather | bytes 1152000 | tf_op jit(solution)/shard_map/all_gather | solution.py:71
  54.7 3.0 %copy.113 = bf16[9,640,80]{1,2,0:T(8,128)(2,1)} copy(bf16[9,640,80]{2,0,1:T(8,128)(2,1)S(1)} %all_gather.12) | data formatting | bytes 1843200 | tf_op jit(solution)/shard_map/all_gather | solution.py:71
  58.0 45.9 %all_gather.14 = bf16[9,640,80]{2,0,1:T(8,128)(2,1)S(1)} all-gather(bf16[9,160,80]{2,0,1:T(8,128)(2,1)S(1)} %copy.123), channel_id=1, replica_groups=mesh['dp'=4,'rows'=8] {'dp'}, dimensions={1}, use_global_device_ids=true | all-gather | bytes 1152000 | tf_op jit(solution)/shard_map/all_gather | solution.py:71
  103.8 3.0 %copy.124 = bf16[9,640,80]{1,2,0:T(8,128)(2,1)} copy(bf16[9,640,80]{2,0,1:T(8,128)(2,1)S(1)} %all_gather.14) | data formatting | bytes 1843200 | tf_op jit(solution)/shard_map/all_gather | solution.py:71
  106.9 2.1 collective-permute-start
  108.9 4.5 %collective-permute-start.1 = (bf16[2,1,64,640]{3,2,1,0:T(8,128)(2,1)S(1)}, bf16[2,1,64,640]{3,2,1,0:T(8,128)(2,1)S(1)}, u32[]{:S(2)}, u32[]{:S(2)}) collective-permute-start(bf16[2,1,64,640]{3,2,1,0:T(8,128)(2,1)S(1)} %copy-done), channel_id=1, source_target_pairs={{1,0},{2,1},{3,2},{4,3},{5,4},{6,5},{7,6},{9,8},{10,9},{11,10},{12... | collective-permute-start | bytes 491528 | tf_op jit(solution)/shard_map/ppermute | solution.py:18
  113.9 12.3 %all-reduce.4 = (f32[2,16]{1,0:T(2,128)S(1)}, f32[2,16]{1,0:T(2,128)S(1)}) all-reduce(f32[2,16]{1,0:T(2,128)S(1)} %reduce_sum.151, f32[2,16]{1,0:T(2,128)S(1)} %reduce_sum.149), channel_id=1, replica_groups=mesh['dp'=4,'rows'=8] {'rows'}, use_global_device_ids=true, to_apply=%region_11.12 | all-reduce | flops 64 | bytes 512 | tf_op jit(solution)/shard_map/psum | solution.py:40
  132.8 1.0 copy.104
  134.8 11.1 %stack.6 = bf16[128,9,640]{2,1,0:T(8,128)(2,1)S(1)} concatenate(bf16[128,1,640]{2,1,0:T(2,128)(2,1)S(1)} %copy.103, bf16[128,1,640]{2,1,0:T(2,128)(2,1)} %copy.104, bf16[128,1,640]{2,1,0:T(2,128)(2,1)} %copy.105, bf16[128,1,640]{2,1,0:T(2,128)(2,1)} %copy.106, bf16[128,1,640]{2,1,0:T(2,128)(2,1)S(1)} %copy.107, bf16[128,1,640]{2,1,0:T(2,128)(2,1)} %copy.108, ...), dimensions={1} | concatenate | bytes 2949120 | tf_op jit(solution)/shard_map/stack | solution.py:70
  145.9 1.8 reshape.88
  147.7 5.1 %fusion.53 = (f32[2,640]{1,0:T(2,128)S(1)}, f32[2,640]{1,0:T(2,128)S(1)}, f32[2,1,64,640]{3,2,0,1:T(8,128)S(1)}) fusion(f32[2,640]{1,0:T(2,128)S(1)} %mul.122, f32[2,640]{1,0:T(2,128)S(1)} %sub.60, bf16[2,1,64,640]{3,2,1,0:T(8,128)(2,1)S(1)} %copy-done.4, f32[640]{0:T(1024)S(1)} %copy-done.6, f32[640]{0:T(1024)S(1)} %copy-done.7, ...), kind=kOutput, calls=%fused_computation.73 | convolution fusion | flops 945108480 | bytes 9364480 | tf_op jit(solution)/shard_map/dot_general | solution.py:76
  153.1 12.0 %all-reduce.3 = (f32[2,16]{1,0:T(2,128)S(1)}, f32[2,16]{1,0:T(2,128)S(1)}, f32[2,16]{1,0:T(2,128)S(1)}, f32[2,16]{1,0:T(2,128)S(1)}) all-reduce(f32[2,16]{1,0:T(2,128)S(1)} %reduce_sum.155, f32[2,16]{1,0:T(2,128)S(1)} %reduce_sum.153, f32[2,16]{1,0:T(2,128)S(1)} %reduce_sum.147, ...), channel_id=1, replica_groups=mesh['dp'=4,'rows'=8] {'rows'}, use_global_device_ids=true, to_apply=%region_17.18 | all-reduce | flops 128 | bytes 1024 | tf_op jit(solution)/shard_map/psum | solution.py:51
  165.5 1.9 collective-permute-start.2
  167.5 4.7 %collective-permute-start.3 = (bf16[2,1,64,640]{3,2,0,1:T(8,128)(2,1)S(1)}, bf16[2,1,64,640]{3,2,0,1:T(8,128)(2,1)S(1)}, u32[]{:S(2)}, u32[]{:S(2)}) collective-permute-start(bf16[2,1,64,640]{3,2,0,1:T(8,128)(2,1)S(1)} %fusion.50), channel_id=1, source_target_pairs={{1,0},{2,1},{3,2},{4,3},{5,4},{6,5},{7,6},{9,8},{10,9},{11,10},{12... | collective-permute-start | bytes 491528 | tf_op jit(solution)/shard_map/ppermute | solution.py:18
  172.8 1.2 collective-permute-done.2
  175.4 1.0 copy.116
  176.4 1.0 copy.117
  180.3 1.0 copy.115
  181.3 1.0 copy.121
  182.3 11.0 %stack.7 = bf16[128,9,640]{2,1,0:T(8,128)(2,1)S(1)} concatenate(bf16[128,1,640]{2,1,0:T(2,128)(2,1)S(1)} %copy.114, bf16[128,1,640]{2,1,0:T(2,128)(2,1)} %copy.115, bf16[128,1,640]{2,1,0:T(2,128)(2,1)} %copy.116, bf16[128,1,640]{2,1,0:T(2,128)(2,1)} %copy.117, bf16[128,1,640]{2,1,0:T(2,128)(2,1)S(1)} %copy.118, bf16[128,1,640]{2,1,0:T(2,128)(2,1)} %copy.119, ...), dimensions={1} | concatenate | bytes 2949120 | tf_op jit(solution)/shard_map/stack | solution.py:70
  193.4 1.8 reshape.92
  195.2 4.9 %fusion.52 = (f32[2,640]{1,0:T(2,128)S(1)}, f32[2,640]{1,0:T(2,128)S(1)}, f32[2,1,64,640]{3,2,0,1:T(8,128)S(1)}) fusion(f32[2,640]{1,0:T(2,128)S(1)} %mul.118, f32[2,640]{1,0:T(2,128)S(1)} %sub.68, bf16[2,1,64,640]{3,2,1,0:T(8,128)(2,1)S(1)} %copy-done.2, f32[640]{0:T(1024)S(1)} %copy-done.8, f32[640]{0:T(1024)S(1)} %copy-done.9, ...), kind=kOutput, calls=%fused_computation.72 | convolution fusion | flops 945108480 | bytes 9364480 | tf_op jit(solution)/shard_map/dot_general | solution.py:76
  200.5 14.6 %all-reduce.2 = (f32[2,16]{1,0:T(2,128)S(1)}, f32[2,16]{1,0:T(2,128)S(1)}) all-reduce(f32[2,16]{1,0:T(2,128)S(1)} %reduce_sum.159, f32[2,16]{1,0:T(2,128)S(1)} %reduce_sum.157), channel_id=1, replica_groups=mesh['dp'=4,'rows'=8] {'rows'}, use_global_device_ids=true, to_apply=%region_23.24 | all-reduce | flops 64 | bytes 512 | tf_op jit(solution)/shard_map/psum | solution.py:51
  (88 shorter events, 15.3 us)
Async XLA Ops:
  6.5 141.2 %all-gather.3.cloned.1.call-start = ((), (), s32[]{:S(2)}) async-start(), calls=%async_computation | async-start | bytes 8294400 | tf_op jit(solution)/shard_map/all_gather | solution.py:72
  54.7 3.1 %copy-start.5 = (bf16[9,160,80]{2,1,0:T(8,128)(2,1)S(1)}, bf16[9,160,80]{2,1,0:T(8,128)(2,1)}, u32[]{:S(2)}) copy-start(bf16[9,160,80]{2,1,0:T(8,128)(2,1)} %param.12) | copy-start | bytes 691204
  57.7 137.5 %all-gather.5.cloned.1.call-start = ((), (), s32[]{:S(2)}) async-start(), calls=%async_computation.1 | async-start | bytes 8294400 | tf_op jit(solution)/shard_map/all_gather | solution.py:72
  103.8 3.0 %copy-start = (bf16[2,1,64,640]{3,2,1,0:T(8,128)(2,1)S(1)}, bf16[2,1,64,640]{3,2,1,0:T(8,128)(2,1)}, u32[]{:S(2)}) copy-start(bf16[2,1,64,640]{3,2,1,0:T(8,128)(2,1)} %param.11) | copy-start | bytes 491524
  103.8 9.6 %copy-start.3 = (bf16[2,1,64,640]{3,2,1,0:T(8,128)(2,1)S(1)}, bf16[2,1,64,640]{3,2,1,0:T(8,128)(2,1)}, u32[]{:S(2)}) copy-start(bf16[2,1,64,640]{3,2,1,0:T(8,128)(2,1)} %param.10) | copy-start | bytes 491524
  106.8 20.0 %copy-start.1 = (bf16[2,1,64,640]{3,2,1,0:T(8,128)(2,1)S(1)}, bf16[2,1,64,640]{3,2,1,0:T(8,128)(2,1)}, u32[]{:S(2)}) copy-start(bf16[2,1,64,640]{3,2,1,0:T(8,128)(2,1)} %param.9) | copy-start | bytes 491524
  106.9 20.4 %collective-permute-start = (bf16[2,1,64,640]{3,2,1,0:T(8,128)(2,1)S(1)}, bf16[2,1,64,640]{3,2,1,0:T(8,128)(2,1)S(1)}, u32[]{:S(2)}, u32[]{:S(2)}) collective-permute-start(bf16[2,1,64,640]{3,2,1,0:T(8,128)(2,1)S(1)} %copy-done), channel_id=1, source_target_pairs={{0,1},{1,2},{2,3},{3,4},{4,5},{5,6},{6,7},{8,9},{9,10},{10,11},{11... | collective-permute-start | bytes 491528 | tf_op jit(solution)/shard_map/ppermute | solution.py:15
  108.9 18.4 %collective-permute-start.1 = (bf16[2,1,64,640]{3,2,1,0:T(8,128)(2,1)S(1)}, bf16[2,1,64,640]{3,2,1,0:T(8,128)(2,1)S(1)}, u32[]{:S(2)}, u32[]{:S(2)}) collective-permute-start(bf16[2,1,64,640]{3,2,1,0:T(8,128)(2,1)S(1)} %copy-done), channel_id=1, source_target_pairs={{1,0},{2,1},{3,2},{4,3},{5,4},{6,5},{7,6},{9,8},{10,9},{11,10},{12... | collective-permute-start | bytes 491528 | tf_op jit(solution)/shard_map/ppermute | solution.py:18
  145.9 1.8 copy-start.4
  145.9 1.8 copy-start.6
  145.9 1.8 copy-start.7
  165.5 8.4 %collective-permute-start.2 = (bf16[2,1,64,640]{3,2,0,1:T(8,128)(2,1)S(1)}, bf16[2,1,64,640]{3,2,0,1:T(8,128)(2,1)S(1)}, u32[]{:S(2)}, u32[]{:S(2)}) collective-permute-start(bf16[2,1,64,640]{3,2,0,1:T(8,128)(2,1)S(1)} %fusion.50), channel_id=1, source_target_pairs={{0,1},{1,2},{2,3},{3,4},{4,5},{5,6},{6,7},{8,9},{9,10},{10,11},{11... | collective-permute-start | bytes 491528 | tf_op jit(solution)/shard_map/ppermute | solution.py:15
  167.5 7.4 %collective-permute-start.3 = (bf16[2,1,64,640]{3,2,0,1:T(8,128)(2,1)S(1)}, bf16[2,1,64,640]{3,2,0,1:T(8,128)(2,1)S(1)}, u32[]{:S(2)}, u32[]{:S(2)}) collective-permute-start(bf16[2,1,64,640]{3,2,0,1:T(8,128)(2,1)S(1)} %fusion.50), channel_id=1, source_target_pairs={{1,0},{2,1},{3,2},{4,3},{5,4},{6,5},{7,6},{9,8},{10,9},{11,10},{12... | collective-permute-start | bytes 491528 | tf_op jit(solution)/shard_map/ppermute | solution.py:18
  193.4 1.8 copy-start.2
  193.4 1.8 copy-start.8
  193.4 1.8 copy-start.9
Sparse Core Ops, SparseCore 0:
  57.9 50.5 all-gather.2
  110.4 50.1 all-gather.4
where the time goes:
time: 225 us; the launch traced here: 223 us
  blocking collectives  132 us (59%)
  local copies, waits for them, and re-layouts  50.2 us (22%)
  between operations  13.8 us (6%)
  starting transfers between devices  13.3 us (6%)
  matrix products  10 us (4%)
    all_gather x2, blocking collectives, conv_backward(): gathered = lax.all_gather(weights, 'dp', axis=1, tiled=True)  92.9 us
    another operation x20, local copies, waits for them, and re-layouts, conv_backward(): stacked = jnp.stack(shifted, axis=1)  36.9 us
    psum x2, blocking collectives, norm_backward(): lax.psum((group_sums(scaled), group_sums(scaled * normed)), 'rows')  26.5 us
    psum x1, blocking collectives, reduced_stats(): lax.psum((group_sums(values), group_sums(values * values)), 'rows')  12.3 us
    dot_general x2, matrix products, conv_backward(): result = jnp.dot(window, flat, preferred_element_type=jnp.float32)  10 us
    ppermute x2, starting transfers between devices, extended(): lax.ppermute(lax.slice_in_dim(block, 0, width, axis=dim), axis, backward)  9.26 us
    all_gather x2, local copies, waits for them, and re-layouts, conv_backward(): gathered = lax.all_gather(weights, 'dp', axis=1, tiled=True)  5.97 us
  transfers between devices with their start and end apart: 6, of which 2 were waited for; matrix products, arithmetic and copies ran while one was open for 23% of the time, Pallas kernels for 0%

commit v1 on v0

--- a/solution.py
+++ b/solution.py
@@ -68,7 +68,12 @@
         ]
         shifted.append(window.reshape(pixels, channels))
     stacked = jnp.stack(shifted, axis=1)
-    gathered = lax.all_gather(weights, "dp", axis=1, tiled=True)
+    ring = [weights]
+    for hop in range(3):
+        ring.append(lax.ppermute(ring[-1], "dp", [(dev, (dev + 1) % 4) for dev in range(4)]))
+    gathered = jnp.roll(
+        jnp.concatenate(ring[::-1], axis=1), (lax.axis_index("dp") + 1) * ring[0].shape[1], axis=1
+    )
     section = lax.all_gather(gathered, "rows", axis=2, tiled=True)
     columns = section.shape[2]
     window = stacked.reshape(pixels, 9 * columns)

time: 225 us -> 200 us (0.89)
  the two profiles are of different devices: /device:TPU:28 before, /device:TPU:4 now
where the time goes in v1:
time: 200 us; the launch traced here: 198 us
  waiting for transfers between devices  67.7 us (34%)
  local copies, waits for them, and re-layouts  44.2 us (22%)
  blocking collectives  40.4 us (20%)
  between operations  13.8 us (7%)
  other arithmetic  11.6 us (6%)
  starting transfers between devices  10.4 us (5%)
  matrix products  9.88 us (5%)
    ppermute x6, waiting for transfers between devices, conv_backward(): lax.ppermute(ring[-1], 'dp', [(dev, (dev + 1) % 4) for dev in range(4)])  60.9 us
    another operation x20, local copies, waits for them, and re-layouts, conv_backward(): stacked = jnp.stack(shifted, axis=1)  36.9 us
    psum x2, blocking collectives, norm_backward(): lax.psum((group_sums(scaled), group_sums(scaled * normed)), 'rows')  25.1 us
    psum x1, blocking collectives, reduced_stats(): lax.psum((group_sums(values), group_sums(values * values)), 'rows')  15.3 us
    dot_general x2, matrix products, conv_backward(): result = jnp.dot(window, flat, preferred_element_type=jnp.float32)  9.88 us
    concatenate x2, other arithmetic, conv_backward(): jnp.roll(jnp.concatenate(ring[::-1], axis=1), (lax.axis_index('dp') + 1)...  9.51 us
    ppermute x2, starting transfers between devices, extended(): lax.ppermute(lax.slice_in_dim(block, block.shape[dim] - width, None, axis...  4.81 us
    ppermute x2, waiting for transfers between devices, extended(): lax.ppermute(lax.slice_in_dim(block, 0, width, axis=dim), axis, backward)  4.14 us
  transfers between devices with their start and end apart: 12, of which 8 were waited for; matrix products, arithmetic and copies ran while one was open for 27% of the time, Pallas kernels for 0%

profile of v1, /device:TPU:4, one launch (start us, length us, event | category | flops | bytes accessed | tf_op | source)
XLA Modules:
  0.0 197.9 jit_solution(2430553926243509620)
XLA Ops:
  7.8 1.6 collective-permute-start.2
  9.4 10.6 %collective-permute-done.2 = bf16[9,160,80]{1,2,0:T(8,128)(2,1)S(1)} collective-permute-done((bf16[9,160,80]{1,2,0:T(8,128)(2,1)S(1)}, bf16[9,160,80]{1,2,0:T(8,128)(2,1)S(1)}, u32[]{:S(2)}, u32[]{:S(2)}) %collective-permute-start.2) | collective-permute-done | bytes 230432 | tf_op jit(solution)/shard_map/ppermute | solution.py:73
  20.0 11.3 %collective-permute-done.3 = bf16[9,160,80]{1,2,0:T(8,128)(2,1)S(1)} collective-permute-done((bf16[9,160,80]{1,2,0:T(8,128)(2,1)S(1)}, bf16[9,160,80]{1,2,0:T(8,128)(2,1)S(1)}, u32[]{:S(2)}, u32[]{:S(2)}) %collective-permute-start.3) | collective-permute-done | bytes 230432 | tf_op jit(solution)/shard_map/ppermute | solution.py:73
  31.3 10.5 %collective-permute-done.4 = bf16[9,160,80]{1,2,0:T(8,128)(2,1)S(1)} collective-permute-done((bf16[9,160,80]{1,2,0:T(8,128)(2,1)S(1)}, bf16[9,160,80]{1,2,0:T(8,128)(2,1)S(1)}, u32[]{:S(2)}, u32[]{:S(2)}) %collective-permute-start.4) | collective-permute-done | bytes 230432 | tf_op jit(solution)/shard_map/ppermute | solution.py:73
  41.8 4.8 %fusion.18 = bf16[9,640,80]{1,2,0:T(8,128)(2,1)} fusion(s32[]{:T(128)S(6)} %select_n.13, bf16[9,160,80]{1,2,0:T(8,128)(2,1)S(1)} %collective-permute-done.4, bf16[9,160,80]{1,2,0:T(8,128)(2,1)S(1)} %collective-permute-done.3, bf16[9,160,80]{1,2,0:T(8,128)(2,1)S(1)} %collective-permute-done.2, bf16[9,160,80]{1,2,0:T(8,128)(2,1)S(1)} %copy.88), kind=kLoop, calls=%fused_computation.40 | loop fusion | flops 7372800 | bytes 1843204 | tf_op jit(solution)/shard_map/jit(_roll_dynamic)/concatenate | solution.py:74
  47.0 9.6 %collective-permute-done.7 = bf16[9,160,80]{1,2,0:T(8,128)(2,1)S(1)} collective-permute-done((bf16[9,160,80]{1,2,0:T(8,128)(2,1)S(1)}, bf16[9,160,80]{1,2,0:T(8,128)(2,1)S(1)}, u32[]{:S(2)}, u32[]{:S(2)}) %collective-permute-start.7) | collective-permute-done | bytes 230432 | tf_op jit(solution)/shard_map/ppermute | solution.py:73
  56.6 9.6 %collective-permute-done.8 = bf16[9,160,80]{1,2,0:T(8,128)(2,1)S(1)} collective-permute-done((bf16[9,160,80]{1,2,0:T(8,128)(2,1)S(1)}, bf16[9,160,80]{1,2,0:T(8,128)(2,1)S(1)}, u32[]{:S(2)}, u32[]{:S(2)}) %collective-permute-start.8) | collective-permute-done | bytes 230432 | tf_op jit(solution)/shard_map/ppermute | solution.py:73
  66.2 9.3 %collective-permute-done.9 = bf16[9,160,80]{1,2,0:T(8,128)(2,1)S(1)} collective-permute-done((bf16[9,160,80]{1,2,0:T(8,128)(2,1)S(1)}, bf16[9,160,80]{1,2,0:T(8,128)(2,1)S(1)}, u32[]{:S(2)}, u32[]{:S(2)}) %collective-permute-start.9) | collective-permute-done | bytes 230432 | tf_op jit(solution)/shard_map/ppermute | solution.py:73
  75.5 4.7 %fusion.11 = bf16[9,640,80]{1,2,0:T(8,128)(2,1)} fusion(s32[]{:T(128)S(6)} %select_n.13, bf16[9,160,80]{1,2,0:T(8,128)(2,1)S(1)} %collective-permute-done.9, bf16[9,160,80]{1,2,0:T(8,128)(2,1)S(1)} %collective-permute-done.8, bf16[9,160,80]{1,2,0:T(8,128)(2,1)S(1)} %collective-permute-done.7, bf16[9,160,80]{1,2,0:T(8,128)(2,1)S(1)} %copy.99), kind=kLoop, calls=%fused_computation.33 | loop fusion | flops 7372800 | bytes 1843204 | tf_op jit(solution)/shard_map/jit(_roll_dynamic)/concatenate | solution.py:74
  80.3 1.9 collective-permute-start.1
  82.2 2.4 %collective-permute-start = (bf16[2,1,64,640]{3,2,1,0:T(8,128)(2,1)S(1)}, bf16[2,1,64,640]{3,2,1,0:T(8,128)(2,1)S(1)}, u32[]{:S(2)}, u32[]{:S(2)}) collective-permute-start(bf16[2,1,64,640]{3,2,1,0:T(8,128)(2,1)S(1)} %copy-done), channel_id=1, source_target_pairs={{0,1},{1,2},{2,3},{3,4},{4,5},{5,6},{6,7},{8,9},{9,10},{10,11},{11... | collective-permute-start | bytes 491528 | tf_op jit(solution)/shard_map/ppermute | solution.py:15
  85.1 15.3 %all-reduce.4 = (f32[2,16]{1,0:T(2,128)S(1)}, f32[2,16]{1,0:T(2,128)S(1)}) all-reduce(f32[2,16]{1,0:T(2,128)S(1)} %reduce_sum.151, f32[2,16]{1,0:T(2,128)S(1)} %reduce_sum.149), channel_id=1, replica_groups=mesh['dp'=4,'rows'=8] {'rows'}, use_global_device_ids=true, to_apply=%region_11.12 | all-reduce | flops 64 | bytes 512 | tf_op jit(solution)/shard_map/psum | solution.py:40
  108.9 11.0 %stack.6 = bf16[128,9,640]{2,1,0:T(8,128)(2,1)S(1)} concatenate(bf16[128,1,640]{2,1,0:T(2,128)(2,1)S(1)} %copy.79, bf16[128,1,640]{2,1,0:T(2,128)(2,1)} %copy.80, bf16[128,1,640]{2,1,0:T(2,128)(2,1)} %copy.81, bf16[128,1,640]{2,1,0:T(2,128)(2,1)} %copy.82, bf16[128,1,640]{2,1,0:T(2,128)(2,1)S(1)} %copy.83, bf16[128,1,640]{2,1,0:T(2,128)(2,1)} %copy.84, ...), dimensions={1} | concatenate | bytes 2949120 | tf_op jit(solution)/shard_map/stack | solution.py:70
  120.0 1.8 reshape.88
  121.8 4.9 %fusion.67 = (f32[2,640]{1,0:T(2,128)S(1)}, f32[2,640]{1,0:T(2,128)S(1)}, f32[2,1,64,640]{3,2,0,1:T(8,128)S(1)}) fusion(f32[2,640]{1,0:T(2,128)S(1)} %mul.126, f32[2,640]{1,0:T(2,128)S(1)} %sub.63, bf16[2,1,64,640]{3,2,1,0:T(8,128)(2,1)S(1)} %copy-done.4, f32[640]{0:T(1024)S(1)} %copy-done.6, f32[640]{0:T(1024)S(1)} %copy-done.7, ...), kind=kOutput, calls=%fused_computation.103 | convolution fusion | flops 945108480 | bytes 9364480 | tf_op jit(solution)/shard_map/dot_general | solution.py:81
  127.1 13.1 %all-reduce.3 = (f32[2,16]{1,0:T(2,128)S(1)}, f32[2,16]{1,0:T(2,128)S(1)}, f32[2,16]{1,0:T(2,128)S(1)}, f32[2,16]{1,0:T(2,128)S(1)}) all-reduce(f32[2,16]{1,0:T(2,128)S(1)} %reduce_sum.155, f32[2,16]{1,0:T(2,128)S(1)} %reduce_sum.153, f32[2,16]{1,0:T(2,128)S(1)} %reduce_sum.147, ...), channel_id=1, replica_groups=mesh['dp'=4,'rows'=8] {'rows'}, use_global_device_ids=true, to_apply=%region_17.19 | all-reduce | flops 128 | bytes 1024 | tf_op jit(solution)/shard_map/psum | solution.py:51
  140.6 1.9 collective-permute-start.6
  142.6 2.4 %collective-permute-start.5 = (bf16[2,1,64,640]{3,2,0,1:T(8,128)(2,1)S(1)}, bf16[2,1,64,640]{3,2,0,1:T(8,128)(2,1)S(1)}, u32[]{:S(2)}, u32[]{:S(2)}) collective-permute-start(bf16[2,1,64,640]{3,2,0,1:T(8,128)(2,1)S(1)} %fusion.64), channel_id=1, source_target_pairs={{0,1},{1,2},{2,3},{3,4},{4,5},{5,6},{6,7},{8,9},{9,10},{10,11},{11... | collective-permute-start | bytes 491528 | tf_op jit(solution)/shard_map/ppermute | solution.py:15
  145.6 4.1 %collective-permute-done.6 = bf16[2,1,64,640]{3,2,0,1:T(8,128)(2,1)S(1)} collective-permute-done((bf16[2,1,64,640]{3,2,0,1:T(8,128)(2,1)S(1)}, bf16[2,1,64,640]{3,2,0,1:T(8,128)(2,1)S(1)}, u32[]{:S(2)}, u32[]{:S(2)}) %collective-permute-start.6) | collective-permute-done | bytes 163872 | tf_op jit(solution)/shard_map/ppermute | solution.py:18
  149.7 2.6 %collective-permute-done.5 = bf16[2,1,64,640]{3,2,0,1:T(8,128)(2,1)S(1)} collective-permute-done((bf16[2,1,64,640]{3,2,0,1:T(8,128)(2,1)S(1)}, bf16[2,1,64,640]{3,2,0,1:T(8,128)(2,1)S(1)}, u32[]{:S(2)}, u32[]{:S(2)}) %collective-permute-start.5) | collective-permute-done | bytes 163872 | tf_op jit(solution)/shard_map/ppermute | solution.py:15
  159.8 11.0 %stack.7 = bf16[128,9,640]{2,1,0:T(8,128)(2,1)S(1)} concatenate(bf16[128,1,640]{2,1,0:T(2,128)(2,1)S(1)} %copy.90, bf16[128,1,640]{2,1,0:T(2,128)(2,1)} %copy.91, bf16[128,1,640]{2,1,0:T(2,128)(2,1)} %copy.92, bf16[128,1,640]{2,1,0:T(2,128)(2,1)} %copy.93, bf16[128,1,640]{2,1,0:T(2,128)(2,1)S(1)} %copy.94, bf16[128,1,640]{2,1,0:T(2,128)(2,1)} %copy.95, ...), dimensions={1} | concatenate | bytes 2949120 | tf_op jit(solution)/shard_map/stack | solution.py:70
  170.9 1.8 reshape.92
  172.7 4.9 %fusion.66 = (f32[2,640]{1,0:T(2,128)S(1)}, f32[2,640]{1,0:T(2,128)S(1)}, f32[2,1,64,640]{3,2,0,1:T(8,128)S(1)}) fusion(f32[2,640]{1,0:T(2,128)S(1)} %mul.122, f32[2,640]{1,0:T(2,128)S(1)} %sub.71, bf16[2,1,64,640]{3,2,1,0:T(8,128)(2,1)S(1)} %copy-done.2, f32[640]{0:T(1024)S(1)} %copy-done.8, f32[640]{0:T(1024)S(1)} %copy-done.9, ...), kind=kOutput, calls=%fused_computation.102 | convolution fusion | flops 945108480 | bytes 9364480 | tf_op jit(solution)/shard_map/dot_general | solution.py:81
  178.0 12.0 %all-reduce.2 = (f32[2,16]{1,0:T(2,128)S(1)}, f32[2,16]{1,0:T(2,128)S(1)}) all-reduce(f32[2,16]{1,0:T(2,128)S(1)} %reduce_sum.159, f32[2,16]{1,0:T(2,128)S(1)} %reduce_sum.157), channel_id=1, replica_groups=mesh['dp'=4,'rows'=8] {'rows'}, use_global_device_ids=true, to_apply=%region_23.25 | all-reduce | flops 64 | bytes 512 | tf_op jit(solution)/shard_map/psum | solution.py:51
  (98 shorter events, 20.8 us)
Async XLA Ops:
  6.5 115.2 %all-gather.3.cloned.1.call-start = ((), (), s32[]{:S(2)}) async-start(), calls=%async_computation | async-start | bytes 8294400 | tf_op jit(solution)/shard_map/all_gather | solution.py:77
  7.8 38.9 %copy-start.5 = (bf16[9,160,80]{2,1,0:T(8,128)(2,1)S(1)}, bf16[9,160,80]{2,1,0:T(8,128)(2,1)}, u32[]{:S(2)}) copy-start(bf16[9,160,80]{2,1,0:T(8,128)(2,1)} %param.14) | copy-start | bytes 691204
  7.8 12.2 %collective-permute-start.2 = (bf16[9,160,80]{1,2,0:T(8,128)(2,1)S(1)}, bf16[9,160,80]{1,2,0:T(8,128)(2,1)S(1)}, u32[]{:S(2)}, u32[]{:S(2)}) collective-permute-start(bf16[9,160,80]{1,2,0:T(8,128)(2,1)S(1)} %copy.88), channel_id=1, source_target_pairs={{0,8},{8,16},{16,24},{24,0},{1,9},{9,17},{17,25},{25,1},{2,10},{10... | collective-permute-start | bytes 691208 | tf_op jit(solution)/shard_map/ppermute | solution.py:73
  20.0 11.3 %collective-permute-start.3 = (bf16[9,160,80]{1,2,0:T(8,128)(2,1)S(1)}, bf16[9,160,80]{1,2,0:T(8,128)(2,1)S(1)}, u32[]{:S(2)}, u32[]{:S(2)}) collective-permute-start(bf16[9,160,80]{1,2,0:T(8,128)(2,1)S(1)} %collective-permute-done.2), channel_id=1, source_target_pairs={{0,8},{8,16},{16,24},{24,0},{1,9},{9,17},{17,25},{25,1},{2,10},{10... | collective-permute-start | bytes 691208 | tf_op jit(solution)/shard_map/ppermute | solution.py:73
  31.3 10.5 %collective-permute-start.4 = (bf16[9,160,80]{1,2,0:T(8,128)(2,1)S(1)}, bf16[9,160,80]{1,2,0:T(8,128)(2,1)S(1)}, u32[]{:S(2)}, u32[]{:S(2)}) collective-permute-start(bf16[9,160,80]{1,2,0:T(8,128)(2,1)S(1)} %collective-permute-done.3), channel_id=1, source_target_pairs={{0,8},{8,16},{16,24},{24,0},{1,9},{9,17},{17,25},{25,1},{2,10},{10... | collective-permute-start | bytes 691208 | tf_op jit(solution)/shard_map/ppermute | solution.py:73
  46.6 126.1 %all-gather.5.cloned.1.call-start = ((), (), s32[]{:S(2)}) async-start(), calls=%async_computation.1 | async-start | bytes 8294400 | tf_op jit(solution)/shard_map/all_gather | solution.py:77
  46.9 33.4 %copy-start = (bf16[2,1,64,640]{3,2,1,0:T(8,128)(2,1)S(1)}, bf16[2,1,64,640]{3,2,1,0:T(8,128)(2,1)}, u32[]{:S(2)}) copy-start(bf16[2,1,64,640]{3,2,1,0:T(8,128)(2,1)} %param.13) | copy-start | bytes 491524
  46.9 37.7 %copy-start.3 = (bf16[2,1,64,640]{3,2,1,0:T(8,128)(2,1)S(1)}, bf16[2,1,64,640]{3,2,1,0:T(8,128)(2,1)}, u32[]{:S(2)}) copy-start(bf16[2,1,64,640]{3,2,1,0:T(8,128)(2,1)} %param.12) | copy-start | bytes 491524
  46.9 54.1 %copy-start.1 = (bf16[2,1,64,640]{3,2,1,0:T(8,128)(2,1)S(1)}, bf16[2,1,64,640]{3,2,1,0:T(8,128)(2,1)}, u32[]{:S(2)}) copy-start(bf16[2,1,64,640]{3,2,1,0:T(8,128)(2,1)} %param.11) | copy-start | bytes 491524
  46.9 9.7 %collective-permute-start.7 = (bf16[9,160,80]{1,2,0:T(8,128)(2,1)S(1)}, bf16[9,160,80]{1,2,0:T(8,128)(2,1)S(1)}, u32[]{:S(2)}, u32[]{:S(2)}) collective-permute-start(bf16[9,160,80]{1,2,0:T(8,128)(2,1)S(1)} %copy.99), channel_id=1, source_target_pairs={{0,8},{8,16},{16,24},{24,0},{1,9},{9,17},{17,25},{25,1},{2,10},{10... | collective-permute-start | bytes 691208 | tf_op jit(solution)/shard_map/ppermute | solution.py:73
  56.6 9.6 %collective-permute-start.8 = (bf16[9,160,80]{1,2,0:T(8,128)(2,1)S(1)}, bf16[9,160,80]{1,2,0:T(8,128)(2,1)S(1)}, u32[]{:S(2)}, u32[]{:S(2)}) collective-permute-start(bf16[9,160,80]{1,2,0:T(8,128)(2,1)S(1)} %collective-permute-done.7), channel_id=1, source_target_pairs={{0,8},{8,16},{16,24},{24,0},{1,9},{9,17},{17,25},{25,1},{2,10},{10... | collective-permute-start | bytes 691208 | tf_op jit(solution)/shard_map/ppermute | solution.py:73
  66.2 9.3 %collective-permute-start.9 = (bf16[9,160,80]{1,2,0:T(8,128)(2,1)S(1)}, bf16[9,160,80]{1,2,0:T(8,128)(2,1)S(1)}, u32[]{:S(2)}, u32[]{:S(2)}) collective-permute-start(bf16[9,160,80]{1,2,0:T(8,128)(2,1)S(1)} %collective-permute-done.8), channel_id=1, source_target_pairs={{0,8},{8,16},{16,24},{24,0},{1,9},{9,17},{17,25},{25,1},{2,10},{10... | collective-permute-start | bytes 691208 | tf_op jit(solution)/shard_map/ppermute | solution.py:73
  80.3 21.2 %collective-permute-start.1 = (bf16[2,1,64,640]{3,2,1,0:T(8,128)(2,1)S(1)}, bf16[2,1,64,640]{3,2,1,0:T(8,128)(2,1)S(1)}, u32[]{:S(2)}, u32[]{:S(2)}) collective-permute-start(bf16[2,1,64,640]{3,2,1,0:T(8,128)(2,1)S(1)} %copy-done), channel_id=1, source_target_pairs={{1,0},{2,1},{3,2},{4,3},{5,4},{6,5},{7,6},{9,8},{10,9},{11,10},{12... | collective-permute-start | bytes 491528 | tf_op jit(solution)/shard_map/ppermute | solution.py:18
  82.2 19.2 %collective-permute-start = (bf16[2,1,64,640]{3,2,1,0:T(8,128)(2,1)S(1)}, bf16[2,1,64,640]{3,2,1,0:T(8,128)(2,1)S(1)}, u32[]{:S(2)}, u32[]{:S(2)}) collective-permute-start(bf16[2,1,64,640]{3,2,1,0:T(8,128)(2,1)S(1)} %copy-done), channel_id=1, source_target_pairs={{0,1},{1,2},{2,3},{3,4},{4,5},{5,6},{6,7},{8,9},{9,10},{10,11},{11... | collective-permute-start | bytes 491528 | tf_op jit(solution)/shard_map/ppermute | solution.py:15
  119.9 1.8 copy-start.4
  120.0 1.8 copy-start.6
  120.0 1.8 copy-start.7
  140.6 9.1 %collective-permute-start.6 = (bf16[2,1,64,640]{3,2,0,1:T(8,128)(2,1)S(1)}, bf16[2,1,64,640]{3,2,0,1:T(8,128)(2,1)S(1)}, u32[]{:S(2)}, u32[]{:S(2)}) collective-permute-start(bf16[2,1,64,640]{3,2,0,1:T(8,128)(2,1)S(1)} %fusion.64), channel_id=1, source_target_pairs={{1,0},{2,1},{3,2},{4,3},{5,4},{6,5},{7,6},{9,8},{10,9},{11,10},{12... | collective-permute-start | bytes 491528 | tf_op jit(solution)/shard_map/ppermute | solution.py:18
  142.6 9.7 %collective-permute-start.5 = (bf16[2,1,64,640]{3,2,0,1:T(8,128)(2,1)S(1)}, bf16[2,1,64,640]{3,2,0,1:T(8,128)(2,1)S(1)}, u32[]{:S(2)}, u32[]{:S(2)}) collective-permute-start(bf16[2,1,64,640]{3,2,0,1:T(8,128)(2,1)S(1)} %fusion.64), channel_id=1, source_target_pairs={{0,1},{1,2},{2,3},{3,4},{4,5},{5,6},{6,7},{8,9},{9,10},{10,11},{11... | collective-permute-start | bytes 491528 | tf_op jit(solution)/shard_map/ppermute | solution.py:15
  170.8 1.8 copy-start.2
  170.8 1.8 copy-start.8
  170.9 1.8 copy-start.9
Sparse Core Ops, SparseCore 0:
  46.7 49.7 all-gather.2
  98.4 53.7 all-gather.4
